TPU v7x, 32 devices: a whole 2x2x4 slice. The times are simulated.
32 devices in a mesh: gx: 8 (over z, x), gy: 2 (over y), gz: 2 (over core).
Axes of the slice: x: 2, y: 2, z: 4, core: 2. Of those that a mesh axis runs over, the one named last changes fastest.
Arguments:
- velocity_term: float32 [32, 64, 256], P('gx', 'gy', 'gz'), may hold values from 0.05 to 0.2
- model_step: float32 [32, 64, 256], P('gx', 'gy', 'gz'), may hold values from -6 to 6
- background: bfloat16 [4, 32, 64, 256], P(None, 'gx', 'gy', 'gz'), may hold values from -6 to 6
- receivers: int32 [3, 256], replicated, may hold values from 0 to 255, as said below
- checkpoints: int32 [16], replicated, may hold values from 0 to 3, as said below
Outputs:
- image: float32 [32, 64, 256], P('gx', 'gy', 'gz')
- traces: float32 [16, 256], replicated
- column_image: float32 [32, 64], P('gx', 'gy')
- wavefield: float32 [32, 64, 256], P('gx', 'gy', 'gz')
Inputs may be any that keep to these rules, and one draw needn't show every extreme that they name: receivers[0] indexes the first lateral dimension (below 32), receivers[1] the second (below 64), receivers[2] depth (below 256). `checkpoints`: never falling over the time steps, beginning at 0 and ending at 3.
All inputs are finite; a program needn't handle non-finite values.
Results may differ from a plain program's by a relative error of at most 0.0003.
Values sent between devices are 32-bit elements; how exact they have to be, the bound alone decides.
A program may use at most 64 MiB of HBM per device.

v0:
```python
import functools

import jax
import jax.numpy as jnp
from jax import lax
from jax.experimental import pallas as pl
from jax.experimental.pallas import tpu as pltpu
from jax.sharding import PartitionSpec as P

near_coef = 4.0 / 3.0
far_coef = -1.0 / 12.0
center_coef = -2.5


def with_halo(block, sides, width, periodic):
    for axis, dim in sides:
        count = lax.axis_size(axis)
        forward = [(i, i + 1) for i in range(count - 1)]
        if periodic:
            forward.append((count - 1, 0))
        backward = [(target, source) for source, target in forward]
        low = lax.ppermute(
            lax.slice_in_dim(block, block.shape[dim] - width, None, axis=dim), axis, forward
        )
        high = lax.ppermute(lax.slice_in_dim(block, 0, width, axis=dim), axis, backward)
        block = jnp.concatenate([low, block, high], axis=dim)
    return block


def along(padded, dim):
    count = padded.shape[dim]
    first = lax.slice_in_dim(padded, 3, count - 1, axis=dim) + lax.slice_in_dim(
        padded, 1, count - 3, axis=dim
    )
    second = lax.slice_in_dim(padded, 4, count, axis=dim) + lax.slice_in_dim(
        padded, 0, count - 4, axis=dim
    )
    return near_coef * first + far_coef * second


def laplace(field):
    side = with_halo(field, (("gx", 0), ("gy", 1)), 2, True)
    deep = with_halo(field, (("gz", 2),), 2, False)
    x_pad = side[:, 2:-2, :]
    y_pad = side[2:-2, :, :]
    return 3.0 * center_coef * field + along(x_pad, 0) + along(y_pad, 1) + along(deep, 2)


def sample_row(samples, field, step, clip_x, clip_y, clip_z, inside):
    values = field[clip_x, clip_y, clip_z] * inside
    return lax.dynamic_update_index_in_dim(samples, values, step, 0)


def on_device(velocity_term, model_step, background, receivers, checkpoints):
    size_x, size_y, size_z = model_step.shape
    steps = checkpoints.shape[0]
    local_x = receivers[0] - lax.axis_index("gx") * size_x
    local_y = receivers[1] - lax.axis_index("gy") * size_y
    local_z = receivers[2] - lax.axis_index("gz") * size_z
    inside = (
        (local_x >= 0)
        & (local_x < size_x)
        & (local_y >= 0)
        & (local_y < size_y)
        & (local_z >= 0)
        & (local_z < size_z)
    )
    inside = inside.astype(jnp.float32)
    clip_x = jnp.clip(local_x, 0, size_x - 1)
    clip_y = jnp.clip(local_y, 0, size_y - 1)
    clip_z = jnp.clip(local_z, 0, size_z - 1)
    zeros = jnp.zeros(model_step.shape, jnp.float32)
    record = jnp.zeros((steps, receivers.shape[1]), jnp.float32)

    def forward(step, carry):
        previous, current, samples = carry
        accel = lax.dynamic_index_in_dim(background, checkpoints[step], 0, keepdims=False).astype(
            jnp.float32
        )
        following = 2.0 * current - previous + velocity_term * laplace(current) + model_step * accel
        samples = sample_row(samples, following, step, clip_x, clip_y, clip_z, inside)
        return (current, following, samples)

    previous, current, record = lax.fori_loop(0, steps, forward, (zeros, zeros, record))
    traces = lax.psum(record, ("gx", "gy", "gz"))

    def adjoint_step(back, carry):
        later_two, later, image = carry
        step = steps - 1 - back
        accel = lax.dynamic_index_in_dim(background, checkpoints[step], 0, keepdims=False).astype(
            jnp.float32
        )
        adjoint = 2.0 * later - later_two + laplace(velocity_term * later)
        inject = lax.dynamic_index_in_dim(traces, step, 0, keepdims=False) * inside
        adjoint = adjoint.at[clip_x, clip_y, clip_z].add(inject)
        return (later, adjoint, image + adjoint * accel)

    later_two, later, image = lax.fori_loop(0, steps, adjoint_step, (zeros, zeros, zeros))
    depth_total = size_z * lax.axis_size("gz")
    column_image = lax.psum(jnp.sum(image, axis=2), "gz") / depth_total
    return (image, traces, column_image, current)


MESH = pl.DeviceIdType.MESH
BLOCK = 4
GROUP = 4


def place_of(p, gxs, gys, gzs):
    q, gz = p // gzs, p % gzs
    per = 2 * gys
    zz, w = q // per, q % per
    w = w + (zz % 2) * (per - 1 - 2 * w)
    xx, yy = w // gys, w % gys
    return 2 * zz + xx, yy + xx * (gys - 1 - 2 * yy), gz


def position_of(gx, gy, gz, gxs, gys, gzs):
    per = 2 * gys
    zz, xx = gx // 2, gx % 2
    w = xx * gys + gy + xx * (gys - 1 - 2 * gy)
    w = w + (zz % 2) * (per - 1 - 2 * w)
    return (zz * per + w) * gzs + gz


def lateral(f, sx, sy, gys):
    rows, lanes = f.shape[1], f.shape[2]
    lane = lax.broadcasted_iota(jnp.int32, f.shape, 2)
    row = lax.broadcasted_iota(jnp.int32, f.shape, 1)
    yl = lane % sy

    def rr(a, k):
        return pltpu.roll(a, k % rows, 1) if k % rows else a

    def lr(a, k):
        return pltpu.roll(a, k % lanes, 2) if k % lanes else a

    gy = row % gys
    up = jnp.where(gy == gys - 1, rr(f, gys - 1), rr(f, -1))
    down = up if gys == 2 else jnp.where(gy == 0, rr(f, 1 - gys), rr(f, 1))
    fu, fd = lr(up, sy), lr(down, -sy)
    y1 = lr(jnp.where(yl >= 1, f, fu), -1) + lr(jnp.where(yl < sy - 1, f, fd), 1)
    y2 = lr(jnp.where(yl >= 2, f, fu), -2) + lr(jnp.where(yl < sy - 2, f, fd), 2)
    xu, xd = rr(f, -gys), rr(f, gys)
    x1 = lr(jnp.where(lane >= sy, f, xu), -sy) + lr(jnp.where(lane < lanes - sy, f, xd), sy)
    x2 = lr(jnp.where(lane >= 2 * sy, f, xu), -2 * sy) + lr(jnp.where(lane < lanes - 2 * sy, f, xd), 2 * sy)
    return near_coef * (x1 + y1) + far_coef * (x2 + y2)


def chain_kernel(
    dims, v_ref, m_ref, bg_ref, rec_ref, ck_ref,
    image_ref, traces_ref, column_ref, wave_ref,
    stage, landed, coef, own_bg, hist, adj, wbuf, img, count, fr, part, tr1, tr2, back_w, back_i, in_w, in_i,
    s_in, r_in, s_c, r_c, s_f, r_f, s_t, r_t, s_w, r_w, s_i, r_i,
):
    gxs, gys, gzs, sx, sy, sz, nck, steps = dims
    n = gxs * gys * gzs
    rows = gxs * gys
    lanes = sx * sy
    nz = sz * gzs // n
    per = sz // nz
    fields = 2 + nck
    gx, gy, gz = lax.axis_index("gx"), lax.axis_index("gy"), lax.axis_index("gz")
    pos = position_of(gx, gy, gz, gxs, gys, gzs)
    my_row = gx * gys + gy
    lo_id = place_of(jnp.maximum(pos - 1, 0), gxs, gys, gzs)
    hi_id = place_of(jnp.minimum(pos + 1, n - 1), gxs, gys, gzs)
    has_lo, has_hi = pos > 0, pos < n - 1
    ext = 3 * nz
    near_halo = 2 * (BLOCK - 1)

    def remote(src, dst, ss, rs, where):
        return pltpu.make_async_remote_copy(
            src_ref=src, dst_ref=dst, send_sem=ss, recv_sem=rs, device_id=where, device_id_type=MESH
        )

    fr[...] = jnp.zeros_like(fr)
    for f in range(1 + nck):
        coef[f, 0:nz] = jnp.zeros((nz, rows, lanes), jnp.float32)
        coef[f, 2 * nz :] = jnp.zeros((nz, rows, lanes), jnp.float32)

    barrier = pltpu.get_barrier_semaphore()

    def greet(p, carry):
        @pl.when(p != pos)
        def _():
            pl.semaphore_signal(barrier, inc=1, device_id=place_of(p, gxs, gys, gzs), device_id_type=MESH)
        return carry

    lax.fori_loop(0, n, greet, 0)

    for f in range(fields):
        if f == 0:
            block = v_ref[...]
        elif f == 1:
            block = m_ref[...]
        else:
            block = bg_ref[f - 2].astype(jnp.float32)
        turned = block.reshape(lanes, sz).T
        stage[:, f * nz : (f + 1) * nz, :] = turned.reshape(per, nz, lanes)
    pl.semaphore_wait(barrier, n - 1)

    slab = fields * nz

    def arrival(row):
        return landed.at[pl.ds(pl.multiple_of(row * slab, nz), slab)]

    def scatter_in(c, carry):
        p = gz * per + c

        @pl.when(p != pos)
        def _():
            remote(stage.at[c], arrival(my_row), s_in.at[c], r_in.at[my_row], place_of(p, gxs, gys, gzs)).start()

        @pl.when(p == pos)
        def _():
            landed[pl.ds(pl.multiple_of(my_row * slab, nz), slab), :] = stage[c]

        return carry

    lax.fori_loop(0, per, scatter_in, 0)

    rec = rec_ref[...]
    rx, ry, rz = rec[0:1], rec[1:2], rec[2:3]
    nrec = rec.shape[1]
    rrow = (rx // sx) * gys + ry // sy
    rlane = (rx % sx) * sy + ry % sy
    rlocal = rz - (pos - 1) * nz
    zr = jnp.where((rlocal >= 0) & (rlocal < ext), rlocal * rows + rrow, -1)
    one_zr = (lax.broadcasted_iota(jnp.int32, (ext * rows, nrec), 0) == zr).astype(jnp.float32)
    one_lane = (lax.broadcasted_iota(jnp.int32, (lanes, nrec), 0) == rlane).astype(jnp.float32)
    counted = lax.dot_general(
        one_zr.astype(jnp.bfloat16), one_lane.astype(jnp.bfloat16), (((1,), (1,)), ((), ())),
        preferred_element_type=jnp.float32,
    )
    count[...] = counted.reshape(ext, rows, lanes)
    hist[0] = jnp.zeros((ext, rows, lanes), jnp.float32)
    hist[1] = jnp.zeros((ext, rows, lanes), jnp.float32)
    adj[steps] = jnp.zeros((ext, rows, lanes), jnp.float32)
    adj[steps + 1] = jnp.zeros((ext, rows, lanes), jnp.float32)
    img[...] = jnp.zeros_like(img)

    owner = pos // per

    def wait_in(row, carry):
        sender = row // gys, row % gys, owner

        @pl.when((row != my_row) | (owner != gz))
        def _():
            remote(stage.at[0], arrival(row), s_in.at[0], r_in.at[row], sender).wait_recv()

        return carry

    lax.fori_loop(0, rows, wait_in, 0)

    def sent_in(c, carry):
        @pl.when(gz * per + c != pos)
        def _():
            remote(stage.at[c], arrival(my_row), s_in.at[c], r_in.at[my_row], lo_id).wait_send()

        return carry

    lax.fori_loop(0, per, sent_in, 0)

    for z in range(nz):
        def plane(f):
            return landed[pl.ds(f * nz + z, rows, stride=slab), :]

        coef[0, nz + z] = plane(0)
        model = plane(1)
        for k in range(nck):
            accel = plane(2 + k)
            own_bg[k, z] = accel
            coef[1 + k, nz + z] = model * accel

    def coef_copies():
        v_lo = remote(coef.at[0, pl.ds(nz, nz)], coef.at[0, pl.ds(2 * nz, nz)], s_c.at[0], r_c.at[0], lo_id)
        m_lo = remote(
            coef.at[pl.ds(1, nck), pl.ds(nz, near_halo)], coef.at[pl.ds(1, nck), pl.ds(2 * nz, near_halo)],
            s_c.at[1], r_c.at[1], lo_id,
        )
        v_hi = remote(coef.at[0, pl.ds(nz, nz)], coef.at[0, pl.ds(0, nz)], s_c.at[2], r_c.at[2], hi_id)
        m_hi = remote(
            coef.at[pl.ds(1, nck), pl.ds(2 * nz - near_halo, near_halo)],
            coef.at[pl.ds(1, nck), pl.ds(nz - near_halo, near_halo)],
            s_c.at[3], r_c.at[3], hi_id,
        )
        return (m_lo, v_lo), (m_hi, v_hi)

    def field_copies(e, newer, older):
        to_lo = [
            remote(a.at[pl.ds(nz, nz)], fr.at[e, 1, i], s_f.at[e, 0, i], r_f.at[e, 1, i], lo_id)
            for i, a in enumerate((newer, older))
        ]
        to_hi = [
            remote(a.at[pl.ds(nz, nz)], fr.at[e, 0, i], s_f.at[e, 1, i], r_f.at[e, 0, i], hi_id)
            for i, a in enumerate((newer, older))
        ]
        return to_lo, to_hi

    def launch(copies):
        to_lo, to_hi = copies

        @pl.when(has_hi)
        def _():
            for c in to_hi:
                c.start()

        @pl.when(has_lo)
        def _():
            for c in to_lo:
                c.start()

    def settle(copies):
        to_lo, to_hi = copies

        @pl.when(has_hi)
        def _():
            for c in to_lo:
                c.wait_recv()
            for c in to_hi:
                c.wait_send()

        @pl.when(has_lo)
        def _():
            for c in to_hi:
                c.wait_recv()
            for c in to_lo:
                c.wait_send()

    def fill(e, newer, older):
        for i, a in enumerate((newer, older)):
            a[0:nz] = fr[e, 0, i]
            a[2 * nz :] = fr[e, 1, i]

    def stencil(ref, at, size):
        f = ref[pl.ds(at, size)]
        first = ref[pl.ds(at + 1, size)] + ref[pl.ds(at - 1, size)]
        second = ref[pl.ds(at + 2, size)] + ref[pl.ds(at - 2, size)]
        return 3.0 * center_coef * f + lateral(f, sx, sy, gys) + near_coef * first + far_coef * second, f

    copies = coef_copies()
    launch(copies)
    settle(copies)

    def forward_block(b, carry):
        for j in range(BLOCK):
            step = b * BLOCK + j
            ck = ck_ref[step]
            lo = 2 * (j + 1)
            for at in range(lo, ext - lo, GROUP):
                size = min(GROUP, ext - lo - at)
                lap, f = stencil(hist.at[step + 1], at, size)
                src = coef[1 + ck, at : at + size]
                hist[step + 2, at : at + size] = (
                    2.0 * f - hist[step, at : at + size] + coef[0, at : at + size] * lap + src
                )
        newer, older = hist.at[(b + 1) * BLOCK + 1], hist.at[(b + 1) * BLOCK]
        moves = field_copies(b, newer, older)
        launch(moves)
        settle(moves)
        fill(b, newer, older)
        return carry

    blocks = steps // BLOCK
    lax.fori_loop(0, blocks, forward_block, 0)

    def send_back(src, dst, ss, rs, slot, g):
        def one(row, carry):
            other = (row != my_row) | (g != gz)

            @pl.when(other)
            def _():
                remote(src.at[row], dst.at[slot], ss.at[row], rs.at[slot], (row // gys, row % gys, g)).start()

            @pl.when(jnp.logical_not(other))
            def _():
                dst[slot] = src[row]

            return carry

        lax.fori_loop(0, rows, one, 0)

    def sent_back(src, dst, ss, rs, g):
        def one(row, carry):
            @pl.when((row != my_row) | (g != gz))
            def _():
                remote(src.at[row], dst.at[0], ss.at[row], rs.at[0], lo_id).wait_send()

            return carry

        lax.fori_loop(0, rows, one, 0)

    def got_back(src, dst, ss, rs, first, number):
        def one(c, carry):
            @pl.when(c + first != pos)
            def _():
                remote(src.at[0], dst.at[c], ss.at[0], rs.at[c], lo_id).wait_recv()

            return carry

        lax.fori_loop(0, number, one, 0)

    near = 4
    far = n // near
    team, seat = pos // near, pos % near

    def trace_sends(src, dst, kind):
        number = near if kind == 0 else far
        mine = seat if kind == 0 else team

        def one(i, carry):
            @pl.when(i != mine)
            def _():
                p = team * near + i if kind == 0 else i * near + seat
                remote(src, dst.at[mine], s_t.at[kind, i], r_t.at[kind, mine], place_of(p, gxs, gys, gzs)).start()

            return carry

        lax.fori_loop(0, number, one, 0)

    def trace_waits(src, dst, kind):
        number = near if kind == 0 else far
        mine = seat if kind == 0 else team

        def one(i, carry):
            @pl.when(i != mine)
            def _():
                remote(src, dst.at[i], s_t.at[kind, i], r_t.at[kind, i], lo_id).wait()

            return carry

        lax.fori_loop(0, number, one, 0)

    def gather_traces():
        picked = one_zr[nz * rows : 2 * nz * rows]
        lines = []
        for t in range(steps):
            table = hist[t + 2, nz : 2 * nz].reshape(nz * rows, lanes)
            at_lane = lax.dot_general(
                table, picked, (((0,), (0,)), ((), ())),
                preferred_element_type=jnp.float32, precision=lax.Precision.HIGHEST,
            )
            lines.append(jnp.sum(at_lane * one_lane, axis=0, keepdims=True))
        return jnp.concatenate(lines, axis=0)

    def adjoint_block(b, carry):
        for j in range(BLOCK):
            step = steps - 1 - b * BLOCK - j
            ck = ck_ref[step]
            lo = 2 * (j + 1)
            wbuf[lo - 2 : ext - lo + 2] = coef[0, lo - 2 : ext - lo + 2] * adj[step + 1, lo - 2 : ext - lo + 2]
            for at in range(lo, ext - lo, GROUP):
                size = min(GROUP, ext - lo - at)
                lap, f = stencil(wbuf, at, size)
                adj[step, at : at + size] = (
                    2.0 * adj[step + 1, at : at + size] - adj[step + 2, at : at + size] + lap
                    + count[at : at + size] * hist[step + 2, at : at + size]
                )
            img[...] += adj[step, nz : 2 * nz] * own_bg[ck]

        @pl.when(b < blocks - 1)
        def _():
            newer, older = adj.at[steps - (b + 1) * BLOCK], adj.at[steps - (b + 1) * BLOCK + 1]
            moves = field_copies(blocks + b, newer, older)
            launch(moves)

            @pl.when(b == 0)
            def _():
                part[0] = gather_traces()
                tr1[seat] = part[0]
                trace_sends(part.at[0], tr1, 0)
                for row in range(rows):
                    for z in range(nz):
                        back_w[row, z : z + 1] = hist[steps + 1, nz + z, row : row + 1]
                send_back(back_w, in_w, s_w, r_w, lax.rem(pos, per), owner)

            @pl.when(b == 1)
            def _():
                trace_waits(part.at[0], tr1, 0)
                total = tr1[0]
                for i in range(1, near):
                    total = total + tr1[i]
                part[1] = total
                tr2[team] = total
                trace_sends(part.at[1], tr2, 1)

            settle(moves)
            fill(blocks + b, newer, older)

        return carry

    lax.fori_loop(0, blocks, adjoint_block, 0)

    for row in range(rows):
        for z in range(nz):
            back_i[row, z : z + 1] = img[z, row : row + 1]
    for g in range(gzs):
        send_back(back_i, in_i, s_i.at[g], r_i, pos, g)

    trace_waits(part.at[1], tr2, 1)
    total = tr2[0]
    for i in range(1, far):
        total = total + tr2[i]
    traces_ref[...] = total
    got_back(back_w, in_w, s_w, r_w, gz * per, per)
    wave_ref[...] = in_w[...].reshape(sz, lanes).T.reshape(sx, sy, sz)
    sent_back(back_w, in_w, s_w, r_w, owner)

    got_back(back_i, in_i, s_i.at[0], r_i, 0, n)
    mine = in_i[pl.ds(gz * per, per)]
    image_ref[...] = mine.reshape(sz, lanes).T.reshape(sx, sy, sz)
    column_ref[...] = jnp.sum(in_i[...].reshape(n * nz, lanes), axis=0, keepdims=True) / (sz * gzs)
    for g in range(gzs):
        sent_back(back_i, in_i, s_i.at[g], r_i, g)


def chain_on_device(sizes, velocity_term, model_step, background, receivers, checkpoints):
    gxs, gys, gzs = sizes
    sx, sy, sz = model_step.shape
    nck, steps, nrec = background.shape[0], checkpoints.shape[0], receivers.shape[1]
    n, rows, lanes = gxs * gys * gzs, gxs * gys, sx * sy
    nz = sz * gzs // n
    per = sz // nz
    ext = 3 * nz
    blocks = steps // BLOCK
    dims = (gxs, gys, gzs, sx, sy, sz, nck, steps)
    f32 = jnp.float32
    dma = pltpu.SemaphoreType.DMA
    vmem = pl.BlockSpec(memory_space=pltpu.VMEM)
    image, traces, column, wave = pl.pallas_call(
        functools.partial(chain_kernel, dims),
        out_shape=(
            jax.ShapeDtypeStruct((sx, sy, sz), f32),
            jax.ShapeDtypeStruct((steps, nrec), f32),
            jax.ShapeDtypeStruct((1, lanes), f32),
            jax.ShapeDtypeStruct((sx, sy, sz), f32),
        ),
        in_specs=[vmem] * 4 + [pl.BlockSpec(memory_space=pltpu.SMEM)],
        out_specs=(vmem,) * 4,
        scratch_shapes=[
            pltpu.VMEM((per, (2 + nck) * nz, lanes), f32),
            pltpu.VMEM((rows * (2 + nck) * nz, lanes), f32),
            pltpu.VMEM((1 + nck, ext, rows, lanes), f32),
            pltpu.VMEM((nck, nz, rows, lanes), f32),
            pltpu.VMEM((steps + 2, ext, rows, lanes), f32),
            pltpu.VMEM((steps + 2, ext, rows, lanes), f32),
            pltpu.VMEM((ext, rows, lanes), f32),
            pltpu.VMEM((nz, rows, lanes), f32),
            pltpu.VMEM((ext, rows, lanes), f32),
            pltpu.VMEM((2 * blocks - 1, 2, 2, nz, rows, lanes), f32),
            pltpu.VMEM((2, steps, nrec), f32),
            pltpu.VMEM((4, steps, nrec), f32),
            pltpu.VMEM((n // 4, steps, nrec), f32),
            pltpu.VMEM((rows, nz, lanes), f32),
            pltpu.VMEM((rows, nz, lanes), f32),
            pltpu.VMEM((per, nz, lanes), f32),
            pltpu.VMEM((n, nz, lanes), f32),
            dma((per,)),
            dma((rows,)),
            dma((4,)),
            dma((4,)),
            dma((2 * blocks - 1, 2, 2)),
            dma((2 * blocks - 1, 2, 2)),
            dma((2, max(4, n // 4))),
            dma((2, max(4, n // 4))),
            dma((rows,)),
            dma((per,)),
            dma((gzs, rows)),
            dma((n,)),
        ],
        compiler_params=pltpu.CompilerParams(
            collective_id=0, has_side_effects=True, vmem_limit_bytes=48 * 1024 * 1024
        ),
    )(velocity_term, model_step, background, receivers, checkpoints)
    return image, traces, column.reshape(sx, sy), wave


def solution(mesh):
    gxs, gys, gzs = mesh.shape["gx"], mesh.shape["gy"], mesh.shape["gz"]
    n = gxs * gys * gzs

    def whole(velocity_term, model_step, background, receivers, checkpoints):
        nx, ny, depth = model_step.shape
        fits = (
            depth % (8 * n) == 0
            and depth // n == 2 * BLOCK
            and gxs % 2 == 0
            and (gxs * gys) % 8 == 0
            and n % 4 == 0
            and (nx // gxs) * (ny // gys) % 128 == 0
            and (ny // gys) % 8 == 0
            and nx // gxs >= 4
            and checkpoints.shape[0] % BLOCK == 0
        )
        body = functools.partial(chain_on_device, (gxs, gys, gzs)) if fits else on_device
        return jax.shard_map(
            body,
            mesh=mesh,
            in_specs=(P("gx", "gy", "gz"), P("gx", "gy", "gz"), P(None, "gx", "gy", "gz"), P(), P()),
            out_specs=(P("gx", "gy", "gz"), P(), P("gx", "gy"), P("gx", "gy", "gz")),
            check_vma=False,
        )(velocity_term, model_step, background, receivers, checkpoints)

    return whole
```

profile of v0, /device:TPU:0, one launch (start us, length us, event | category | flops | bytes accessed | tf_op | source)
XLA Modules:
  0.0 81.3 jit_solution(16536089498099412087)
XLA Ops:
  0.6 0.0 copy-start
  0.6 0.9 %copy-done = bf16[4,4,32,128]{3,2,1,0:T(8,128)(2,1)S(1)} copy-done((bf16[4,4,32,128]{3,2,1,0:T(8,128)(2,1)S(1)}, bf16[4,4,32,128]{3,2,1,0:T(8,128)(2,1)}, u32[]{:S(2)}) %copy-start) | copy-done | bytes 131096
  1.5 0.0 copy-start.1
  1.5 0.8 %copy-done.1 = f32[4,32,128]{2,1,0:T(8,128)S(1)} copy-done((f32[4,32,128]{2,1,0:T(8,128)S(1)}, f32[4,32,128]{2,1,0:T(8,128)}, u32[]{:S(2)}) %copy-start.1) | copy-done | bytes 65560
  2.4 0.0 copy-start.2
  2.4 0.8 %copy-done.2 = f32[4,32,128]{2,1,0:T(8,128)S(1)} copy-done((f32[4,32,128]{2,1,0:T(8,128)S(1)}, f32[4,32,128]{2,1,0:T(8,128)}, u32[]{:S(2)}) %copy-start.2) | copy-done | bytes 65560
  3.2 0.0 copy-start.3
  3.2 0.7 copy-done.3
  3.9 0.0 copy-start.4
  3.9 0.7 copy-done.4
  4.6 73.1 %shard_map.84 = (f32[4,32,128]{2,1,0:T(8,128)S(1)}, f32[16,256]{1,0:T(8,128)S(1)}, f32[1,128]{1,0:T(1,128)S(1)}, f32[4,32,128]{2,1,0:T(8,128)S(1)}) custom-call(f32[4,32,128]{2,1,0:T(8,128)S(1)} %copy-done.1, f32[4,32,128]{2,1,0:T(8,128)S(1)} %copy-done.2, bf16[4,4,32,128]{3,2,1,0:T(8,128)(2,1)S(1)} %copy-done, s32[3,256]{1,0:T(4,128)S(1)} %copy-done.3, ...), custom_call_target="tpu_custom_call" | custom-call | tf_op jit(solution)/shard_map/pallas_call | solution.py:531
  77.6 0.5 broadcast.3
  78.1 0.7 reduce.3
  78.8 0.7 reshape.11
  79.5 0.6 copy.12
  80.1 0.6 copy.13
  80.7 0.6 copy.14
Async XLA Ops:
  0.6 0.9 %copy-start = (bf16[4,4,32,128]{3,2,1,0:T(8,128)(2,1)S(1)}, bf16[4,4,32,128]{3,2,1,0:T(8,128)(2,1)}, u32[]{:S(2)}) copy-start(bf16[4,4,32,128]{3,2,1,0:T(8,128)(2,1)} %bg_ref.1) | copy-start | bytes 393220
  1.5 0.8 %copy-start.1 = (f32[4,32,128]{2,1,0:T(8,128)S(1)}, f32[4,32,128]{2,1,0:T(8,128)}, u32[]{:S(2)}) copy-start(f32[4,32,128]{2,1,0:T(8,128)} %v_ref.1) | copy-start | bytes 196612
  2.4 0.8 %copy-start.2 = (f32[4,32,128]{2,1,0:T(8,128)S(1)}, f32[4,32,128]{2,1,0:T(8,128)}, u32[]{:S(2)}) copy-start(f32[4,32,128]{2,1,0:T(8,128)} %m_ref.1) | copy-start | bytes 196612
  3.2 0.7 copy-start.3
  3.9 0.7 copy-start.4
where the time goes:
time: 82 us; the launch traced here: 81.3 us
  Pallas kernels  73.1 us (89%)
  local copies, waits for them, and re-layouts  6.96 us (8%)
    pallas_call x1, Pallas kernels, chain_on_device(): pl.pallas_call(functools.partial(chain_kernel, dims), out_shape=(jax.Shap...  73.1 us
    unnamed x13, local copies, waits for them, and re-layouts  5.78 us

commit v1 on v0

v1 whole, which is shorter than its diff:
```python
import functools

import jax
import jax.numpy as jnp
from jax import lax
from jax.experimental import pallas as pl
from jax.experimental.pallas import tpu as pltpu
from jax.sharding import PartitionSpec as P

near_coef = 4.0 / 3.0
far_coef = -1.0 / 12.0
center_coef = -2.5


def with_halo(block, sides, width, periodic):
    for axis, dim in sides:
        count = lax.axis_size(axis)
        forward = [(i, i + 1) for i in range(count - 1)]
        if periodic:
            forward.append((count - 1, 0))
        backward = [(target, source) for source, target in forward]
        low = lax.ppermute(
            lax.slice_in_dim(block, block.shape[dim] - width, None, axis=dim), axis, forward
        )
        high = lax.ppermute(lax.slice_in_dim(block, 0, width, axis=dim), axis, backward)
        block = jnp.concatenate([low, block, high], axis=dim)
    return block


def along(padded, dim):
    count = padded.shape[dim]
    first = lax.slice_in_dim(padded, 3, count - 1, axis=dim) + lax.slice_in_dim(
        padded, 1, count - 3, axis=dim
    )
    second = lax.slice_in_dim(padded, 4, count, axis=dim) + lax.slice_in_dim(
        padded, 0, count - 4, axis=dim
    )
    return near_coef * first + far_coef * second


def laplace(field):
    side = with_halo(field, (("gx", 0), ("gy", 1)), 2, True)
    deep = with_halo(field, (("gz", 2),), 2, False)
    x_pad = side[:, 2:-2, :]
    y_pad = side[2:-2, :, :]
    return 3.0 * center_coef * field + along(x_pad, 0) + along(y_pad, 1) + along(deep, 2)


def sample_row(samples, field, step, clip_x, clip_y, clip_z, inside):
    values = field[clip_x, clip_y, clip_z] * inside
    return lax.dynamic_update_index_in_dim(samples, values, step, 0)


def on_device(velocity_term, model_step, background, receivers, checkpoints):
    size_x, size_y, size_z = model_step.shape
    steps = checkpoints.shape[0]
    local_x = receivers[0] - lax.axis_index("gx") * size_x
    local_y = receivers[1] - lax.axis_index("gy") * size_y
    local_z = receivers[2] - lax.axis_index("gz") * size_z
    inside = (
        (local_x >= 0)
        & (local_x < size_x)
        & (local_y >= 0)
        & (local_y < size_y)
        & (local_z >= 0)
        & (local_z < size_z)
    )
    inside = inside.astype(jnp.float32)
    clip_x = jnp.clip(local_x, 0, size_x - 1)
    clip_y = jnp.clip(local_y, 0, size_y - 1)
    clip_z = jnp.clip(local_z, 0, size_z - 1)
    zeros = jnp.zeros(model_step.shape, jnp.float32)
    record = jnp.zeros((steps, receivers.shape[1]), jnp.float32)

    def forward(step, carry):
        previous, current, samples = carry
        accel = lax.dynamic_index_in_dim(background, checkpoints[step], 0, keepdims=False).astype(
            jnp.float32
        )
        following = 2.0 * current - previous + velocity_term * laplace(current) + model_step * accel
        samples = sample_row(samples, following, step, clip_x, clip_y, clip_z, inside)
        return (current, following, samples)

    previous, current, record = lax.fori_loop(0, steps, forward, (zeros, zeros, record))
    traces = lax.psum(record, ("gx", "gy", "gz"))

    def adjoint_step(back, carry):
        later_two, later, image = carry
        step = steps - 1 - back
        accel = lax.dynamic_index_in_dim(background, checkpoints[step], 0, keepdims=False).astype(
            jnp.float32
        )
        adjoint = 2.0 * later - later_two + laplace(velocity_term * later)
        inject = lax.dynamic_index_in_dim(traces, step, 0, keepdims=False) * inside
        adjoint = adjoint.at[clip_x, clip_y, clip_z].add(inject)
        return (later, adjoint, image + adjoint * accel)

    later_two, later, image = lax.fori_loop(0, steps, adjoint_step, (zeros, zeros, zeros))
    depth_total = size_z * lax.axis_size("gz")
    column_image = lax.psum(jnp.sum(image, axis=2), "gz") / depth_total
    return (image, traces, column_image, current)


MESH = pl.DeviceIdType.MESH
BLOCK = 4
GROUP = 4


def place_of(p, gxs, gys, gzs):
    q, gz = p // gzs, p % gzs
    per = 2 * gys
    zz, w = q // per, q % per
    w = w + (zz % 2) * (per - 1 - 2 * w)
    xx, yy = w // gys, w % gys
    return 2 * zz + xx, yy + xx * (gys - 1 - 2 * yy), gz


def position_of(gx, gy, gz, gxs, gys, gzs):
    per = 2 * gys
    zz, xx = gx // 2, gx % 2
    w = xx * gys + gy + xx * (gys - 1 - 2 * gy)
    w = w + (zz % 2) * (per - 1 - 2 * w)
    return (zz * per + w) * gzs + gz


def lane_roll(a, k):
    return pltpu.roll(a, k % a.shape[-1], a.ndim - 1)


def row_roll(a, k):
    return pltpu.roll(a, k % a.shape[-2], a.ndim - 2)


def quarter_owner(k, gy):
    base = (k % 2) * 2 + k // 2
    return base + gy * (2 - 4 * (k % 2))


class Plane:
    def __init__(self, rows, lanes):
        half = lanes // 2
        lane = lax.broadcasted_iota(jnp.int32, (rows, lanes), 1)
        y = lane % half
        self.half = half
        self.first, self.second = y < 1, y < 2
        self.last, self.before = y >= half - 1, y >= half - 2
        self.even = lane < half
        self.odd_quarter = lane % half >= half // 2

    def swap_quarters(self, a):
        quarter = self.half // 2
        return jnp.where(self.odd_quarter, lane_roll(a, quarter), lane_roll(a, -quarter))

    def join(self, low, high):
        return (
            jnp.where(self.odd_quarter, high, low),
            self.swap_quarters(jnp.where(self.odd_quarter, low, high)),
        )

    def split(self, f0, f1):
        t = self.swap_quarters(f1)
        return jnp.where(self.odd_quarter, t, f0), jnp.where(self.odd_quarter, f0, t)

    def along_y(self, f, r):
        near = lane_roll(jnp.where(self.first, r, f), -1) + lane_roll(jnp.where(self.last, r, f), 1)
        far = lane_roll(jnp.where(self.second, r, f), -2) + lane_roll(jnp.where(self.before, r, f), 2)
        return near, far

    def lateral(self, f):
        r = lane_roll(f, self.half)
        near, far = self.along_y(f, r)
        f0, f1, r0, r1 = f[:, 0], f[:, 1], r[:, 0], r[:, 1]
        near = near + r + jnp.stack(
            [jnp.where(self.even, row_roll(r1, 1), r1), jnp.where(self.even, r0, row_roll(r0, -1))], axis=1
        )
        far = far + jnp.stack([f1 + row_roll(f1, 1), f0 + row_roll(f0, -1)], axis=1)
        return near, far


def chain_kernel(
    dims, v_hbm, m_hbm, bg_hbm, rec_hbm, ck_hbm,
    image_ref, traces_ref, column_ref, wave_ref,
    v_in, m_in, bg_in, rec_in, ck_in,
    stage, landed, vel, src, far, own_bg, hist, adj, wbuf, img, count, part, tr1, tr2,
    back_w, back_i, back_c, in_w, in_i, in_c,
    s_0, s_in, r_in, s_c, r_c, s_f, r_f, s_t, r_t, s_w, r_w, s_i, r_i, s_k, r_k,
):
    gxs, gys, gzs, sx, sy, sz, nck, steps = dims
    n = gxs * gys * gzs
    rows = gxs * gys
    lanes = sx * sy
    nz = sz * gzs // n
    per = sz // nz
    fields = 2 + nck
    gx, gy, gz = lax.axis_index("gx"), lax.axis_index("gy"), lax.axis_index("gz")
    pos = position_of(gx, gy, gz, gxs, gys, gzs)
    my_row = gx * gys + gy
    lo_id = place_of(jnp.maximum(pos - 1, 0), gxs, gys, gzs)
    hi_id = place_of(jnp.minimum(pos + 1, n - 1), gxs, gys, gzs)
    has_lo, has_hi = pos > 0, pos < n - 1
    ext = 3 * nz
    f32 = jnp.float32
    tile = (gxs, lanes)

    def remote(src_ref, dst_ref, ss, rs, where):
        return pltpu.make_async_remote_copy(
            src_ref=src_ref, dst_ref=dst_ref, send_sem=ss, recv_sem=rs, device_id=where, device_id_type=MESH
        )

    barrier = pltpu.get_barrier_semaphore()

    def greet(p, carry):
        @pl.when(p != pos)
        def _():
            pl.semaphore_signal(barrier, inc=1, device_id=place_of(p, gxs, gys, gzs), device_id_type=MESH)
        return carry

    loads = [
        pltpu.make_async_copy(a, b, s_0.at[i])
        for i, (a, b) in enumerate(
            ((v_hbm, v_in), (m_hbm, m_in), (bg_hbm, bg_in), (rec_hbm, rec_in), (ck_hbm, ck_in))
        )
    ]
    for load in loads:
        load.start()
    lax.fori_loop(0, n, greet, 0)

    plane = Plane(gxs, lanes)

    @pl.when(jnp.logical_not(has_lo))
    def _():
        vel[0:nz] = jnp.zeros((nz, 2) + tile, f32)
        for k in range(nck):
            src[k, 0:nz] = jnp.zeros((nz, 2) + tile, f32)
        for t in range(steps):
            hist[t, 0:nz] = jnp.zeros((nz, 2) + tile, f32)
            adj[t, 0:nz] = jnp.zeros((nz, 2) + tile, f32)

    @pl.when(jnp.logical_not(has_hi))
    def _():
        vel[2 * nz :] = jnp.zeros((nz, 2) + tile, f32)
        for k in range(nck):
            src[k, 2 * nz :] = jnp.zeros((nz, 2) + tile, f32)
        for t in range(steps):
            hist[t, 2 * nz :] = jnp.zeros((nz, 2) + tile, f32)
            adj[t, 2 * nz :] = jnp.zeros((nz, 2) + tile, f32)

    for load in loads[:3]:
        load.wait()
    for f in range(fields):
        pieces = []
        for k in range(sx):
            x = quarter_owner(k, gy)
            if f == 0:
                pieces.append(v_in[x])
            elif f == 1:
                pieces.append(m_in[x])
            else:
                pieces.append(bg_in[f - 2, x].astype(f32))
        turned = jnp.concatenate(pieces, axis=0).T
        stage[:, f * nz : (f + 1) * nz, :] = turned.reshape(per, nz, lanes)
    pl.semaphore_wait(barrier, n - 1)

    slab = fields * nz

    def arrival(row):
        return landed.at[pl.ds(pl.multiple_of(row * slab, nz), slab)]

    def scatter_in(c, carry):
        p = gz * per + c

        @pl.when(p != pos)
        def _():
            remote(stage.at[c], arrival(my_row), s_in.at[c], r_in.at[my_row], place_of(p, gxs, gys, gzs)).start()

        @pl.when(p == pos)
        def _():
            landed[pl.ds(pl.multiple_of(my_row * slab, nz), slab), :] = stage[c]

        return carry

    lax.fori_loop(0, per, scatter_in, 0)

    for load in loads[3:]:
        load.wait()
    rec = rec_in[...]
    rx, ry, rz = rec[0:1], rec[1:2], rec[2:3]
    nrec = rec.shape[1]
    rlane = (rx % 2) * (lanes // 2) + ry
    rlocal = rz - (pos - 1) * nz
    zr = jnp.where((rlocal >= 0) & (rlocal < ext), (rlocal * 2 + (rx % sx) // 2) * gxs + rx // sx, -1)
    one_zr = (lax.broadcasted_iota(jnp.int32, (ext * rows, nrec), 0) == zr).astype(f32)
    one_lane = (lax.broadcasted_iota(jnp.int32, (lanes, nrec), 0) == rlane).astype(f32)
    counted = lax.dot_general(
        one_zr.astype(jnp.bfloat16), one_lane.astype(jnp.bfloat16), (((1,), (1,)), ((), ())),
        preferred_element_type=f32,
    )
    count[...] = counted.reshape((ext, 2) + tile)
    img[...] = jnp.zeros_like(img)

    owner = pos // per

    def wait_in(row, carry):
        sender = row // gys, row % gys, owner

        @pl.when((row != my_row) | (owner != gz))
        def _():
            remote(stage.at[0], arrival(row), s_in.at[0], r_in.at[row], sender).wait_recv()

        return carry

    lax.fori_loop(0, rows, wait_in, 0)

    def gathered(f, z):
        low = landed[pl.ds(f * nz + z, gxs, stride=gys * slab), :]
        high = landed[pl.ds(slab + f * nz + z, gxs, stride=gys * slab), :]
        return plane.join(low, high)

    for z in range(nz):
        vs = gathered(0, z)
        ms = gathered(1, z)
        for c in range(2):
            vel[nz + z, c] = far_coef * vs[c]
        for k in range(nck):
            accel = gathered(2 + k, z)
            for c in range(2):
                own_bg[k, z, c] = accel[c]
                src[k, nz + z, c] = ms[c] * accel[c]

    halo = 2 * BLOCK
    soon, rest = halo // 4, halo // 2

    def pairs(make):
        return make(0, lo_id), make(1, hi_id)

    def ranges(side, near_at, size):
        at = nz - near_at - size if side else near_at
        return pl.ds(nz + at, size), pl.ds(at if side else 2 * nz + at, size)

    def first_coefs(side, where):
        a, b = ranges(side, 0, soon)
        c, d = ranges(side, soon, soon)
        i = 3 * side
        j = 3 * (1 - side)
        return [
            remote(src.at[0, c], src.at[0, d], s_c.at[i], r_c.at[j], where),
            remote(src.at[:, a], src.at[:, b], s_c.at[i + 1], r_c.at[j + 1], where),
            remote(vel.at[a], vel.at[b], s_c.at[i + 2], r_c.at[j + 2], where),
        ]

    def later_coefs(side, where):
        a, b = ranges(side, soon, halo - soon)
        c, _ = ranges(side, 2 * soon, soon)
        d, _ = ranges(side, soon, rest)
        i = 6 + 3 * side
        j = 6 + 3 * (1 - side)
        return [
            remote(src.at[0, c], far.at[1 - side, 0, pl.ds(0, soon)], s_c.at[i], r_c.at[j], where),
            remote(src.at[pl.ds(1, nck - 1), d], far.at[1 - side, pl.ds(1, nck - 1)], s_c.at[i + 1], r_c.at[j + 1], where),
            remote(vel.at[a], vel.at[b], s_c.at[i + 2], r_c.at[j + 2], where),
        ]

    def newer_copies(e, newer):
        def make(side, where):
            a, b = ranges(side, 0, nz)
            return [remote(newer.at[a], newer.at[b], s_f.at[e, side, 0], r_f.at[e, 1 - side, 0], where)]
        return pairs(make)

    def older_copies(e, older):
        def make(side, where):
            a, b = ranges(side, 2, halo - 4)
            return [remote(older.at[a], older.at[b], s_f.at[e, side, 1], r_f.at[e, 1 - side, 1], where)]
        return pairs(make)

    def launch(copies):
        to_lo, to_hi = copies

        @pl.when(has_hi)
        def _():
            for c in to_hi:
                c.start()

        @pl.when(has_lo)
        def _():
            for c in to_lo:
                c.start()

    def settle(copies):
        to_lo, to_hi = copies

        @pl.when(has_hi)
        def _():
            for c in to_lo:
                c.wait_recv()
            for c in to_hi:
                c.wait_send()

        @pl.when(has_lo)
        def _():
            for c in to_hi:
                c.wait_recv()
            for c in to_lo:
                c.wait_send()

    opening, closing = pairs(first_coefs), pairs(later_coefs)
    launch(opening)
    launch(closing)

    def sent_in(c, carry):
        @pl.when(gz * per + c != pos)
        def _():
            remote(stage.at[c], arrival(my_row), s_in.at[c], r_in.at[my_row], lo_id).wait_send()

        return carry

    lax.fori_loop(0, per, sent_in, 0)
    settle(opening)

    def spread(ref, at, size):
        f = ref[pl.ds(at, size)]
        near, wide = plane.lateral(f)
        near = near + (ref[pl.ds(at + 1, size)] + ref[pl.ds(at - 1, size)])
        wide = wide + (ref[pl.ds(at + 2, size)] + ref[pl.ds(at - 2, size)])
        return wide - 16.0 * near + 90.0 * f, f

    def groups(width):
        lo, hi = nz - width, 2 * nz + width
        for at in range(lo, hi, GROUP):
            yield at, min(GROUP, hi - at)

    def forward_step(t, width):
        k = ck_in[t]
        for at, size in groups(width):
            here = pl.ds(at, size)
            lap, f = spread(hist.at[t - 1], at, size)
            value = 2.0 * f + vel[here] * lap + src[k, here]
            if t > 1:
                value = value - hist[t - 2, here]
            hist[t, here] = value

    def adjoint_step(t, width):
        k = ck_in[t]
        first = t == steps - 1
        if not first:
            for at, size in groups(width + 2):
                here = pl.ds(at, size)
                wbuf[here] = vel[here] * adj[t + 1, here]
        for at, size in groups(width):
            here = pl.ds(at, size)
            value = count[here] * hist[t, here]
            if not first:
                lap, _ = spread(wbuf, at, size)
                value = value + lap + 2.0 * adj[t + 1, here]
                if t < steps - 2:
                    value = value - adj[t + 2, here]
            adj[t, here] = value
        img[...] = img[...] + adj[t, nz : 2 * nz] * own_bg[k]

    blocks = steps // BLOCK

    for z in range(nz - 2 * soon, 2 * nz + 2 * soon):
        for c in range(2):
            hist[0, z, c] = src[0, z, c]
    forward_step(1, 2)
    older = older_copies(0, hist.at[1])
    launch(older)
    forward_step(2, 0)
    newer = newer_copies(0, hist.at[2])
    launch(newer)
    settle(closing)

    @pl.when(has_lo)
    def _():
        src[0, nz - halo + 2 : nz - halo + 2 + soon] = far[0, 0, 0:soon]
        src[1:, nz - halo + 2 : nz - soon] = far[0, 1:]

    @pl.when(has_hi)
    def _():
        src[0, 2 * nz + 2 * soon : 2 * nz + 3 * soon] = far[1, 0, 0:soon]
        src[1:, 2 * nz + soon : 2 * nz + 3 * soon] = far[1, 1:]

    settle(older)
    settle(newer)

    def forward_block(b):
        t = b * BLOCK - 1
        for j in range(BLOCK - 1):
            forward_step(t + j, halo - 2 * (j + 1))
        older = older_copies(b, hist.at[t + BLOCK - 2])
        launch(older)
        forward_step(t + BLOCK - 1, 0)
        newer = newer_copies(b, hist.at[t + BLOCK - 1])
        launch(newer)
        settle(older)
        settle(newer)

    for b in range(1, blocks):
        forward_block(b)

    def send_back(src_ref, dst, ss, rs, slot, g):
        def one(row, carry):
            other = (row != my_row) | (g != gz)
            piece = src_ref.at[pl.ds(pl.multiple_of(row * nz, nz), nz)]

            @pl.when(other)
            def _():
                remote(piece, dst.at[slot], ss.at[row], rs.at[slot], (row // gys, row % gys, g)).start()

            @pl.when(jnp.logical_not(other))
            def _():
                dst[slot] = piece[...]

            return carry

        lax.fori_loop(0, rows, one, 0)

    def sent_back(src_ref, dst, ss, rs, g):
        def one(row, carry):
            @pl.when((row != my_row) | (g != gz))
            def _():
                remote(src_ref.at[pl.ds(0, nz)], dst.at[0], ss.at[row], rs.at[0], lo_id).wait_send()

            return carry

        lax.fori_loop(0, rows, one, 0)

    def got_back(src_ref, dst, ss, rs, first, number):
        def one(c, carry):
            @pl.when(c + first != pos)
            def _():
                remote(src_ref.at[pl.ds(0, nz)], dst.at[c], ss.at[0], rs.at[c], lo_id).wait_recv()

            return carry

        lax.fori_loop(0, number, one, 0)

    near = 4
    apart = n // near
    team, seat = pos // near, pos % near

    def trace_sends(src_ref, dst, kind):
        number = near if kind == 0 else apart
        mine = seat if kind == 0 else team

        def one(i, carry):
            @pl.when(i != mine)
            def _():
                p = team * near + i if kind == 0 else i * near + seat
                remote(src_ref, dst.at[mine], s_t.at[kind, i], r_t.at[kind, mine], place_of(p, gxs, gys, gzs)).start()

            return carry

        lax.fori_loop(0, number, one, 0)

    def trace_waits(src_ref, dst, kind):
        number = near if kind == 0 else apart
        mine = seat if kind == 0 else team

        def one(i, carry):
            @pl.when(i != mine)
            def _():
                remote(src_ref, dst.at[i], s_t.at[kind, i], r_t.at[kind, i], lo_id).wait()

            return carry

        lax.fori_loop(0, number, one, 0)

    def gather_traces():
        picked = one_zr[nz * rows : 2 * nz * rows]
        lane_pick = one_lane.astype(jnp.bfloat16)
        lines = []
        for t in range(steps):
            table = hist[t, nz : 2 * nz].reshape(nz * rows, lanes)
            at_row = jnp.zeros((nz * rows, nrec), f32)
            for _ in range(3):
                piece = table.astype(jnp.bfloat16)
                at_row = at_row + jnp.dot(piece, lane_pick, preferred_element_type=f32)
                table = table - piece.astype(f32)
            lines.append(jnp.sum(at_row * picked, axis=0, keepdims=True))
        return jnp.concatenate(lines, axis=0)

    def give_back(read, dst):
        for z in range(nz):
            for g, value in enumerate(plane.split(*read(z))):
                dst[pl.ds(g * nz + z, gxs, stride=gys * nz), :] = value

    last = steps - 1
    forward_step(last, halo - 2)
    adjoint_step(last, halo - 2)
    adjoint_step(last - 1, halo - 4)
    adjoint_step(last - 2, halo - 6)
    older = older_copies(blocks, adj.at[last - 2])
    launch(older)
    adjoint_step(last - 3, 0)
    newer = newer_copies(blocks, adj.at[last - 3])
    launch(newer)
    give_back(lambda z: (hist[last, nz + z, 0], hist[last, nz + z, 1]), back_w)
    send_back(back_w, in_w, s_w, r_w, lax.rem(pos, per), owner)
    part[0] = gather_traces()
    tr1[seat] = part[0]
    trace_sends(part.at[0], tr1, 0)
    settle(older)
    settle(newer)

    def trace_relay():
        trace_waits(part.at[0], tr1, 0)
        total = tr1[0]
        for i in range(1, near):
            total = total + tr1[i]
        part[1] = total
        tr2[team] = total
        trace_sends(part.at[1], tr2, 1)

    def adjoint_block(b):
        t = last - BLOCK * b
        for j in range(BLOCK - 1):
            adjoint_step(t - j, halo - 2 * (j + 1))
        if b == blocks - 1:
            adjoint_step(t - BLOCK + 1, 0)
            return
        older = older_copies(blocks + b, adj.at[t - BLOCK + 2])
        launch(older)
        adjoint_step(t - BLOCK + 1, 0)
        newer = newer_copies(blocks + b, adj.at[t - BLOCK + 1])
        launch(newer)
        if b == 1:
            trace_relay()
        settle(older)
        settle(newer)

    for b in range(1, blocks):
        adjoint_block(b)

    give_back(lambda z: (img[z, 0], img[z, 1]), back_i)
    send_back(back_i, in_i, s_i, r_i, lax.rem(pos, per), owner)
    sums = [img[0, c] for c in range(2)]
    for z in range(1, nz):
        sums = [sums[c] + img[z, c] for c in range(2)]
    for g, value in enumerate(plane.split(*sums)):
        for i in range(gxs):
            back_c[i * gys + g] = value[i : i + 1]

    def send_sums(i, carry):
        row, g = i // gzs, i % gzs
        other = (row != my_row) | (g != gz)

        @pl.when(other)
        def _():
            remote(back_c.at[row], in_c.at[pos], s_k.at[i], r_k.at[pos], (row // gys, row % gys, g)).start()

        @pl.when(jnp.logical_not(other))
        def _():
            in_c[pos] = back_c[row]

        return carry

    lax.fori_loop(0, n, send_sums, 0)

    trace_waits(part.at[1], tr2, 1)
    total = tr2[0]
    for i in range(1, apart):
        total = total + tr2[i]
    traces_ref[...] = total

    def put_out(buffer, out_ref):
        turned = buffer[...].reshape(sz, lanes).T
        for k in range(sx):
            out_ref[quarter_owner(k, gy)] = turned[k * sy : (k + 1) * sy]

    got_back(back_w, in_w, s_w, r_w, gz * per, per)
    put_out(in_w, wave_ref)
    sent_back(back_w, in_w, s_w, r_w, owner)

    got_back(back_i, in_i, s_i, r_i, gz * per, per)
    put_out(in_i, image_ref)

    def got_sums(i, carry):
        @pl.when(i != pos)
        def _():
            remote(back_c.at[0], in_c.at[i], s_k.at[0], r_k.at[i], lo_id).wait_recv()

        return carry

    lax.fori_loop(0, n, got_sums, 0)
    depth = in_c[0]
    for i in range(1, n):
        depth = depth + in_c[i]
    depth = depth / (sz * gzs)
    for k in range(sx):
        column_ref[pl.ds(quarter_owner(k, gy), 1), :] = depth[:, k * sy : (k + 1) * sy]
    sent_back(back_i, in_i, s_i, r_i, owner)

    def sent_sums(i, carry):
        @pl.when((i // gzs != my_row) | (i % gzs != gz))
        def _():
            remote(back_c.at[0], in_c.at[0], s_k.at[i], r_k.at[0], lo_id).wait_send()

        return carry

    lax.fori_loop(0, n, sent_sums, 0)


def store_kernel(*refs):
    count = len(refs) // 2
    ins, outs, sems = refs[:count], refs[count : 2 * count], refs[2 * count]
    copies = [pltpu.make_async_copy(a, b, sems.at[i]) for i, (a, b) in enumerate(zip(ins, outs))]
    for copy in copies:
        copy.start()
    for copy in copies:
        copy.wait()


def chain_on_device(sizes, velocity_term, model_step, background, receivers, checkpoints):
    gxs, gys, gzs = sizes
    sx, sy, sz = model_step.shape
    nck, steps, nrec = background.shape[0], checkpoints.shape[0], receivers.shape[1]
    n, rows, lanes = gxs * gys * gzs, gxs * gys, sx * sy
    nz = sz * gzs // n
    per = sz // nz
    ext = 3 * nz
    blocks = steps // BLOCK
    halo = 2 * BLOCK
    dims = (gxs, gys, gzs, sx, sy, sz, nck, steps)
    f32 = jnp.float32
    dma = pltpu.SemaphoreType.DMA
    vmem = pl.BlockSpec(memory_space=pltpu.VMEM)
    hbm = pl.BlockSpec(memory_space=pltpu.HBM)
    tile = (2, gxs, lanes)
    shapes = (
        jax.ShapeDtypeStruct((sx, sy, sz), f32),
        jax.ShapeDtypeStruct((steps, nrec), f32),
        jax.ShapeDtypeStruct((sx, sy), f32),
        jax.ShapeDtypeStruct((sx, sy, sz), f32),
    )
    results = pl.pallas_call(
        functools.partial(chain_kernel, dims),
        out_shape=shapes,
        in_specs=[hbm] * 5,
        out_specs=(vmem,) * 4,
        scratch_shapes=[
            pltpu.VMEM(velocity_term.shape, f32),
            pltpu.VMEM(model_step.shape, f32),
            pltpu.VMEM(background.shape, background.dtype),
            pltpu.VMEM(receivers.shape, receivers.dtype),
            pltpu.SMEM(checkpoints.shape, checkpoints.dtype),
            pltpu.VMEM((per, (2 + nck) * nz, lanes), f32),
            pltpu.VMEM((rows * (2 + nck) * nz, lanes), f32),
            pltpu.VMEM((ext,) + tile, f32),
            pltpu.VMEM((nck, ext) + tile, f32),
            pltpu.VMEM((2, nck, halo // 2) + tile, f32),
            pltpu.VMEM((nck, nz) + tile, f32),
            pltpu.VMEM((steps, ext) + tile, f32),
            pltpu.VMEM((steps, ext) + tile, f32),
            pltpu.VMEM((ext,) + tile, f32),
            pltpu.VMEM((nz,) + tile, f32),
            pltpu.VMEM((ext,) + tile, f32),
            pltpu.VMEM((2, steps, nrec), f32),
            pltpu.VMEM((4, steps, nrec), f32),
            pltpu.VMEM((n // 4, steps, nrec), f32),
            pltpu.VMEM((rows * nz, lanes), f32),
            pltpu.VMEM((rows * nz, lanes), f32),
            pltpu.VMEM((rows, 1, lanes), f32),
            pltpu.VMEM((per, nz, lanes), f32),
            pltpu.VMEM((per, nz, lanes), f32),
            pltpu.VMEM((n, 1, lanes), f32),
            dma((5,)),
            dma((per,)),
            dma((rows,)),
            dma((12,)),
            dma((12,)),
            dma((2 * blocks - 1, 2, 2)),
            dma((2 * blocks - 1, 2, 2)),
            dma((2, max(4, n // 4))),
            dma((2, max(4, n // 4))),
            dma((rows,)),
            dma((per,)),
            dma((rows,)),
            dma((per,)),
            dma((n,)),
            dma((n,)),
        ],
        compiler_params=pltpu.CompilerParams(
            collective_id=0, has_side_effects=True, vmem_limit_bytes=48 * 1024 * 1024
        ),
    )(velocity_term, model_step, background, receivers, checkpoints)
    return pl.pallas_call(
        store_kernel,
        out_shape=shapes,
        in_specs=[vmem] * 4,
        out_specs=(hbm,) * 4,
        scratch_shapes=[dma((4,))],
    )(*results)


def solution(mesh):
    gxs, gys, gzs = mesh.shape["gx"], mesh.shape["gy"], mesh.shape["gz"]
    n = gxs * gys * gzs

    def whole(velocity_term, model_step, background, receivers, checkpoints):
        nx, ny, depth = model_step.shape
        fits = (
            depth % (8 * n) == 0
            and depth // n == 2 * BLOCK
            and gxs == 8
            and gys == 2
            and n % 4 == 0
            and nx // gxs == 4
            and (nx // gxs) * (ny // gys) == 128
            and checkpoints.shape[0] == 4 * BLOCK
        )
        body = functools.partial(chain_on_device, (gxs, gys, gzs)) if fits else on_device
        return jax.shard_map(
            body,
            mesh=mesh,
            in_specs=(P("gx", "gy", "gz"), P("gx", "gy", "gz"), P(None, "gx", "gy", "gz"), P(), P()),
            out_specs=(P("gx", "gy", "gz"), P(), P("gx", "gy"), P("gx", "gy", "gz")),
            check_vma=False,
        )(velocity_term, model_step, background, receivers, checkpoints)

    return whole
```

time: 82 us -> 71.6 us (0.87)
  Pallas kernels: 73.1 us -> 64.3 us
    pallas_call x1 -> x2, Pallas kernels: 73.1 us -> 64.3 us  [the longest x1 62.7 us: chain_on_device(): pl.pallas_call(functools.partial(chain_kernel, dims), out_shape=shapes, i...]
    unnamed x13 -> x18, local copies, waits for them, and re-layouts: 5.78 us -> 6.34 us
where the time goes in v1:
time: 71.6 us; the launch traced here: 71.3 us
  Pallas kernels  64.3 us (90%)
  local copies, waits for them, and re-layouts  6.34 us (9%)
    pallas_call x1, Pallas kernels, chain_on_device(): pl.pallas_call(functools.partial(chain_kernel, dims), out_shape=shapes, i...  62.7 us
    unnamed x18, local copies, waits for them, and re-layouts  6.34 us
    pallas_call x1, Pallas kernels, chain_on_device(): pl.pallas_call(store_kernel, out_shape=shapes, in_specs=[vmem] * 4, out_s...  1.59 us

profile of v1, /device:TPU:0, one launch (start us, length us, event | category | flops | bytes accessed | tf_op | source)
XLA Modules:
  0.0 71.3 jit_solution(9767501302431017452)
XLA Ops:
  0.6 0.0 copy-start
  0.6 0.9 %copy-done = bf16[4,4,32,128]{3,2,1,0:T(8,128)(2,1)S(1)} copy-done((bf16[4,4,32,128]{3,2,1,0:T(8,128)(2,1)S(1)}, bf16[4,4,32,128]{3,2,1,0:T(8,128)(2,1)}, u32[]{:S(2)}) %copy-start) | copy-done | bytes 131096
  1.5 0.0 copy-start.3
  1.5 0.8 %copy-done.3 = f32[4,32,128]{2,1,0:T(8,128)S(1)} copy-done((f32[4,32,128]{2,1,0:T(8,128)S(1)}, f32[4,32,128]{2,1,0:T(8,128)}, u32[]{:S(2)}) %copy-start.3) | copy-done | bytes 65560
  2.4 0.0 copy-start.4
  2.4 0.8 %copy-done.4 = f32[4,32,128]{2,1,0:T(8,128)S(1)} copy-done((f32[4,32,128]{2,1,0:T(8,128)S(1)}, f32[4,32,128]{2,1,0:T(8,128)}, u32[]{:S(2)}) %copy-start.4) | copy-done | bytes 65560
  3.2 0.0 copy-start.6
  3.2 0.7 copy-done.6
  3.9 0.0 copy-start.8
  3.9 0.7 copy-done.8
  4.6 62.7 %shard_map.84 = (f32[4,32,128]{2,1,0:T(8,128)S(1)}, f32[16,256]{1,0:T(8,128)S(1)}, f32[4,32]{1,0:T(4,128)S(1)}, f32[4,32,128]{2,1,0:T(8,128)S(1)}) custom-call(f32[4,32,128]{2,1,0:T(8,128)S(1)} %copy-done.3, f32[4,32,128]{2,1,0:T(8,128)S(1)} %copy-done.4, bf16[4,4,32,128]{3,2,1,0:T(8,128)(2,1)S(1)} %copy-done, s32[3,256]{1,0:T(4,128)S(1)} %copy-done.6, ...), custom_call_target="tpu_custom_call" | custom-call | tf_op jit(solution)/shard_map/pallas_call | solution.py:735
  67.2 0.0 copy-start.1
  67.3 0.6 copy-done.1
  67.9 0.0 copy-start.2
  67.9 0.6 copy-done.2
  68.5 0.0 copy-start.5
  68.5 0.6 copy-done.5
  69.1 0.0 copy-start.7
  69.1 0.6 copy-done.7
  69.7 1.6 %shard_map.85 = (f32[4,32,128]{2,1,0:T(8,128)}, f32[16,256]{1,0:T(8,128)}, f32[4,32]{1,0:T(4,128)}, f32[4,32,128]{2,1,0:T(8,128)}) custom-call(f32[4,32,128]{2,1,0:T(8,128)} %copy-done.1, f32[16,256]{1,0:T(8,128)} %copy-done.5, f32[4,32]{1,0:T(4,128)} %copy-done.7, f32[4,32,128]{2,1,0:T(8,128)} %copy-done.2), custom_call_target="tpu_custom_call" | custom-call | tf_op jit(solution)/shard_map/pallas_call | solution.py:786
Async XLA Ops:
  0.6 0.9 %copy-start = (bf16[4,4,32,128]{3,2,1,0:T(8,128)(2,1)S(1)}, bf16[4,4,32,128]{3,2,1,0:T(8,128)(2,1)}, u32[]{:S(2)}) copy-start(bf16[4,4,32,128]{3,2,1,0:T(8,128)(2,1)} %bg_hbm.1) | copy-start | bytes 393220
  1.5 0.8 %copy-start.3 = (f32[4,32,128]{2,1,0:T(8,128)S(1)}, f32[4,32,128]{2,1,0:T(8,128)}, u32[]{:S(2)}) copy-start(f32[4,32,128]{2,1,0:T(8,128)} %v_hbm.1) | copy-start | bytes 196612
  2.4 0.8 %copy-start.4 = (f32[4,32,128]{2,1,0:T(8,128)S(1)}, f32[4,32,128]{2,1,0:T(8,128)}, u32[]{:S(2)}) copy-start(f32[4,32,128]{2,1,0:T(8,128)} %m_hbm.1) | copy-start | bytes 196612
  3.2 0.7 copy-start.6
  3.9 0.7 copy-start.8
  67.2 0.6 copy-start.1
  67.9 0.6 copy-start.2
  68.5 0.6 copy-start.5
  69.1 0.6 copy-start.7

commit v2 on v1

--- a/solution.py
+++ b/solution.py
@@ -140,10 +140,7 @@
     def __init__(self, rows, lanes):
         half = lanes // 2
         lane = lax.broadcasted_iota(jnp.int32, (rows, lanes), 1)
-        y = lane % half
         self.half = half
-        self.first, self.second = y < 1, y < 2
-        self.last, self.before = y >= half - 1, y >= half - 2
         self.even = lane < half
         self.odd_quarter = lane % half >= half // 2
 
@@ -161,27 +158,30 @@
         t = self.swap_quarters(f1)
         return jnp.where(self.odd_quarter, t, f0), jnp.where(self.odd_quarter, f0, t)
 
-    def along_y(self, f, r):
-        near = lane_roll(jnp.where(self.first, r, f), -1) + lane_roll(jnp.where(self.last, r, f), 1)
-        far = lane_roll(jnp.where(self.second, r, f), -2) + lane_roll(jnp.where(self.before, r, f), 2)
-        return near, far
-
-    def lateral(self, f):
-        r = lane_roll(f, self.half)
-        near, far = self.along_y(f, r)
-        f0, f1, r0, r1 = f[:, 0], f[:, 1], r[:, 0], r[:, 1]
-        near = near + r + jnp.stack(
-            [jnp.where(self.even, row_roll(r1, 1), r1), jnp.where(self.even, r0, row_roll(r0, -1))], axis=1
-        )
-        far = far + jnp.stack([f1 + row_roll(f1, 1), f0 + row_roll(f0, -1)], axis=1)
-        return near, far
+    def taps(self):
+        lanes = 2 * self.half
+        shape = (2 * lanes, 2 * lanes)
+        i, j = lax.broadcasted_iota(jnp.int32, shape, 0) % lanes, lax.broadcasted_iota(jnp.int32, shape, 1)
+        across = (i - j + lanes) % lanes == self.half
+        shift = (j - i + lanes) % self.half
+        same = (i < self.half) == (j < self.half)
+        near = same & ((shift == 1) | (shift == self.half - 1))
+        far = same & ((shift == 2) | (shift == self.half - 2))
+        beside = jnp.where(near, -16.0, 0.0) + jnp.where(far, 1.0, 0.0)
+        return (jnp.where(j < lanes, beside, 0.0) + jnp.where(across, -16.0, 0.0)).astype(jnp.bfloat16)
+
+    def lateral(self, f, y_sum, other):
+        x0, x1, f0, f1 = other[:, 0], other[:, 1], f[:, 0], f[:, 1]
+        low = jnp.where(self.even, row_roll(x1, 1), x1) + (f1 + row_roll(f1, 1))
+        high = jnp.where(self.even, x0, row_roll(x0, -1)) + (f0 + row_roll(f0, -1))
+        return y_sum + jnp.stack([low, high], axis=1)
 
 
 def chain_kernel(
     dims, v_hbm, m_hbm, bg_hbm, rec_hbm, ck_hbm,
     image_ref, traces_ref, column_ref, wave_ref,
     v_in, m_in, bg_in, rec_in, ck_in,
-    stage, landed, vel, src, far, own_bg, hist, adj, wbuf, img, count, part, tr1, tr2,
+    stage, landed, vel, src, far, own_bg, hist, adj, wbuf, taps, mixed, img, count, part, tr1, tr2,
     back_w, back_i, back_c, in_w, in_i, in_c,
     s_0, s_in, r_in, s_c, r_c, s_f, r_f, s_t, r_t, s_w, r_w, s_i, r_i, s_k, r_k,
 ):
@@ -297,6 +297,7 @@
     )
     count[...] = counted.reshape((ext, 2) + tile)
     img[...] = jnp.zeros_like(img)
+    taps[...] = plane.taps()
 
     owner = pos // per
 
@@ -416,12 +417,23 @@
     lax.fori_loop(0, per, sent_in, 0)
     settle(opening)
 
+    def lateral_sums(ref, width):
+        size = nz + 2 * width
+        f = ref[pl.ds(nz - width, size)].reshape(size * rows, lanes)
+        top = f.astype(jnp.bfloat16)
+        low = (f - top.astype(f32)).astype(jnp.bfloat16)
+        mixed[pl.ds((nz - width) * rows, size * rows)] = jnp.dot(
+            jnp.concatenate([top, low], axis=1), taps[...], preferred_element_type=f32
+        )
+
     def spread(ref, at, size):
         f = ref[pl.ds(at, size)]
-        near, wide = plane.lateral(f)
-        near = near + (ref[pl.ds(at + 1, size)] + ref[pl.ds(at - 1, size)])
-        wide = wide + (ref[pl.ds(at + 2, size)] + ref[pl.ds(at - 2, size)])
-        return wide - 16.0 * near + 90.0 * f, f
+        m = pl.ds(at * rows, size * rows)
+        shape = (size, 2) + tile
+        near = ref[pl.ds(at + 1, size)] + ref[pl.ds(at - 1, size)]
+        wide = ref[pl.ds(at + 2, size)] + ref[pl.ds(at - 2, size)]
+        flat = plane.lateral(f, mixed[m, 0:lanes].reshape(shape), mixed[m, lanes : 2 * lanes].reshape(shape))
+        return flat + wide - 16.0 * near + 90.0 * f, f
 
     def groups(width):
         lo, hi = nz - width, 2 * nz + width
@@ -430,6 +442,7 @@
 
     def forward_step(t, width):
         k = ck_in[t]
+        lateral_sums(hist.at[t - 1], width)
         for at, size in groups(width):
             here = pl.ds(at, size)
             lap, f = spread(hist.at[t - 1], at, size)
@@ -445,6 +458,7 @@
             for at, size in groups(width + 2):
                 here = pl.ds(at, size)
                 wbuf[here] = vel[here] * adj[t + 1, here]
+            lateral_sums(wbuf, width)
         for at, size in groups(width):
             here = pl.ds(at, size)
             value = count[here] * hist[t, here]
@@ -752,6 +766,8 @@
             pltpu.VMEM((steps, ext) + tile, f32),
             pltpu.VMEM((steps, ext) + tile, f32),
             pltpu.VMEM((ext,) + tile, f32),
+            pltpu.VMEM((2 * lanes, 2 * lanes), jnp.bfloat16),
+            pltpu.VMEM((ext * rows, 2 * lanes), f32),
             pltpu.VMEM((nz,) + tile, f32),
             pltpu.VMEM((ext,) + tile, f32),
             pltpu.VMEM((2, steps, nrec), f32),
@@ -782,13 +798,17 @@
         compiler_params=pltpu.CompilerParams(
             collective_id=0, has_side_effects=True, vmem_limit_bytes=48 * 1024 * 1024
         ),
-    )(velocity_term, model_step, background, receivers, checkpoints)
+    )(*(
+        pltpu.with_memory_space_constraint(a, pltpu.HBM)
+        for a in (velocity_term, model_step, background, receivers, checkpoints)
+    ))
     return pl.pallas_call(
         store_kernel,
         out_shape=shapes,
         in_specs=[vmem] * 4,
         out_specs=(hbm,) * 4,
         scratch_shapes=[dma((4,))],
+        compiler_params=pltpu.CompilerParams(vmem_limit_bytes=1024 * 1024),
     )(*results)
 
 

time: 71.6 us -> 59.1 us (0.83)
  local copies, waits for them, and re-layouts: 6.34 us -> 0 us
  Pallas kernels: 64.3 us -> 58.3 us
    unnamed x18 -> x0, local copies, waits for them, and re-layouts: 6.34 us -> none
    pallas_call x1, Pallas kernels: 62.7 us -> 57.6 us  [chain_on_device(): pl.pallas_call(functools.partial(chain_kernel, dims), out_shape=shapes, i...]
    pallas_call x1, Pallas kernels: 1.59 us -> 0.7 us  [chain_on_device(): pl.pallas_call(store_kernel, out_shape=shapes, in_specs=[vmem] * 4, out_s...]
where the time goes in v2:
time: 59.1 us; the launch traced here: 58.9 us
  Pallas kernels  58.3 us (99%)
  between operations  0.64 us (1%)
    pallas_call x1, Pallas kernels, chain_on_device(): pl.pallas_call(functools.partial(chain_kernel, dims), out_shape=shapes, i...  57.6 us

profile of v2, /device:TPU:0, one launch (start us, length us, event | category | flops | bytes accessed | tf_op | source)
XLA Modules:
  0.0 58.9 jit_solution(7196497195364783967)
XLA Ops:
  0.6 57.6 %shard_map.84 = (f32[4,32,128]{2,1,0:T(8,128)S(1)}, f32[16,256]{1,0:T(8,128)S(1)}, f32[4,32]{1,0:T(4,128)S(1)}, f32[4,32,128]{2,1,0:T(8,128)S(1)}) custom-call(f32[4,32,128]{2,1,0:T(8,128)} %v_hbm.1, f32[4,32,128]{2,1,0:T(8,128)} %m_hbm.1, bf16[4,4,32,128]{3,2,1,0:T(8,128)(2,1)} %bg_hbm.1, s32[3,256]{1,0:T(4,128)} %rec_hbm.1, s32[16]{0:T(128)} %ck_hbm.1), custom_call_target="tpu_custom_call" | custom-call | tf_op jit(solution)/shard_map/pallas_call | solution.py:749
  58.2 0.7 %shard_map.85 = (f32[4,32,128]{2,1,0:T(8,128)}, f32[16,256]{1,0:T(8,128)}, f32[4,32]{1,0:T(4,128)}, f32[4,32,128]{2,1,0:T(8,128)}) custom-call(f32[4,32,128]{2,1,0:T(8,128)S(1)} %get-tuple-element.8.refs_0_, f32[16,256]{1,0:T(8,128)S(1)} %get-tuple-element.9.refs_1_, f32[4,32]{1,0:T(4,128)S(1)} %get-tuple-element.10.refs_2_, ...), custom_call_target="tpu_custom_call" | custom-call | tf_op jit(solution)/shard_map/pallas_call | solution.py:805

commit v3 on v2

--- a/solution.py
+++ b/solution.py
@@ -182,7 +182,7 @@
     image_ref, traces_ref, column_ref, wave_ref,
     v_in, m_in, bg_in, rec_in, ck_in,
     stage, landed, vel, src, far, own_bg, hist, adj, wbuf, taps, mixed, img, count, part, tr1, tr2,
-    back_w, back_i, back_c, in_w, in_i, in_c,
+    back_w, back_i, in_w, in_i, in_c,
     s_0, s_in, r_in, s_c, r_c, s_f, r_f, s_t, r_t, s_w, r_w, s_i, r_i, s_k, r_k,
 ):
     gxs, gys, gzs, sx, sy, sz, nck, steps = dims
@@ -266,7 +266,8 @@
     def arrival(row):
         return landed.at[pl.ds(pl.multiple_of(row * slab, nz), slab)]
 
-    def scatter_in(c, carry):
+    def scatter_in(i, carry):
+        c = lax.rem(i + my_row, per)
         p = gz * per + c
 
         @pl.when(p != pos)
@@ -512,7 +513,8 @@
         forward_block(b)
 
     def send_back(src_ref, dst, ss, rs, slot, g):
-        def one(row, carry):
+        def one(i, carry):
+            row = lax.rem(my_row + rows // 2 + i, rows)
             other = (row != my_row) | (g != gz)
             piece = src_ref.at[pl.ds(pl.multiple_of(row * nz, nz), nz)]
 
@@ -647,29 +649,6 @@
 
     give_back(lambda z: (img[z, 0], img[z, 1]), back_i)
     send_back(back_i, in_i, s_i, r_i, lax.rem(pos, per), owner)
-    sums = [img[0, c] for c in range(2)]
-    for z in range(1, nz):
-        sums = [sums[c] + img[z, c] for c in range(2)]
-    for g, value in enumerate(plane.split(*sums)):
-        for i in range(gxs):
-            back_c[i * gys + g] = value[i : i + 1]
-
-    def send_sums(i, carry):
-        row, g = i // gzs, i % gzs
-        other = (row != my_row) | (g != gz)
-
-        @pl.when(other)
-        def _():
-            remote(back_c.at[row], in_c.at[pos], s_k.at[i], r_k.at[pos], (row // gys, row % gys, g)).start()
-
-        @pl.when(jnp.logical_not(other))
-        def _():
-            in_c[pos] = back_c[row]
-
-        return carry
-
-    lax.fori_loop(0, n, send_sums, 0)
-
     trace_waits(part.at[1], tr2, 1)
     total = tr2[0]
     for i in range(1, apart):
@@ -684,34 +663,30 @@
     got_back(back_w, in_w, s_w, r_w, gz * per, per)
     put_out(in_w, wave_ref)
     sent_back(back_w, in_w, s_w, r_w, owner)
+    sent_back(back_i, in_i, s_i, r_i, owner)
 
     got_back(back_i, in_i, s_i, r_i, gz * per, per)
+    in_c[gz] = jnp.sum(in_i[...].reshape(sz, lanes), axis=0, keepdims=True)
+
+    def sums_to(i, where):
+        return remote(in_c.at[gz], in_c.at[gz], s_k.at[i], r_k.at[gz], (gx, gy, where))
+
+    def sums_from(i):
+        return remote(in_c.at[i], in_c.at[i], s_k.at[i], r_k.at[i], (gx, gy, i))
+
+    for step in range(1, gzs):
+        sums_to(step, lax.rem(gz + step, gzs)).start()
     put_out(in_i, image_ref)
-
-    def got_sums(i, carry):
-        @pl.when(i != pos)
-        def _():
-            remote(back_c.at[0], in_c.at[i], s_k.at[0], r_k.at[i], lo_id).wait_recv()
-
-        return carry
-
-    lax.fori_loop(0, n, got_sums, 0)
+    for step in range(1, gzs):
+        sums_from(lax.rem(gz + step, gzs)).wait_recv()
     depth = in_c[0]
-    for i in range(1, n):
+    for i in range(1, gzs):
         depth = depth + in_c[i]
     depth = depth / (sz * gzs)
     for k in range(sx):
         column_ref[pl.ds(quarter_owner(k, gy), 1), :] = depth[:, k * sy : (k + 1) * sy]
-    sent_back(back_i, in_i, s_i, r_i, owner)
-
-    def sent_sums(i, carry):
-        @pl.when((i // gzs != my_row) | (i % gzs != gz))
-        def _():
-            remote(back_c.at[0], in_c.at[0], s_k.at[i], r_k.at[0], lo_id).wait_send()
-
-        return carry
-
-    lax.fori_loop(0, n, sent_sums, 0)
+    for step in range(1, gzs):
+        sums_to(step, lax.rem(gz + step, gzs)).wait_send()
 
 
 def store_kernel(*refs):
@@ -775,10 +750,9 @@
             pltpu.VMEM((n // 4, steps, nrec), f32),
             pltpu.VMEM((rows * nz, lanes), f32),
             pltpu.VMEM((rows * nz, lanes), f32),
-            pltpu.VMEM((rows, 1, lanes), f32),
             pltpu.VMEM((per, nz, lanes), f32),
             pltpu.VMEM((per, nz, lanes), f32),
-            pltpu.VMEM((n, 1, lanes), f32),
+            pltpu.VMEM((gzs, 1, lanes), f32),
             dma((5,)),
             dma((per,)),
             dma((rows,)),
@@ -792,8 +766,8 @@
             dma((per,)),
             dma((rows,)),
             dma((per,)),
-            dma((n,)),
-            dma((n,)),
+            dma((gzs,)),
+            dma((gzs,)),
         ],
         compiler_params=pltpu.CompilerParams(
             collective_id=0, has_side_effects=True, vmem_limit_bytes=48 * 1024 * 1024

time: 59.1 us -> 57.2 us (0.968)
  Pallas kernels: 58.3 us -> 56.4 us
    pallas_call x1, Pallas kernels: 57.6 us -> 55.7 us  [chain_on_device(): pl.pallas_call(functools.partial(chain_kernel, dims), out_shape=shapes, i...]
where the time goes in v3:
time: 57.2 us; the launch traced here: 57 us
  Pallas kernels  56.4 us (99%)
  between operations  0.64 us (1%)
    pallas_call x1, Pallas kernels, chain_on_device(): pl.pallas_call(functools.partial(chain_kernel, dims), out_shape=shapes, i...  55.7 us

profile of v3, /device:TPU:0, one launch (start us, length us, event | category | flops | bytes accessed | tf_op | source)
XLA Modules:
  0.0 57.0 jit_solution(18143529453721215419)
XLA Ops:
  0.6 55.7 %shard_map.84 = (f32[4,32,128]{2,1,0:T(8,128)S(1)}, f32[16,256]{1,0:T(8,128)S(1)}, f32[4,32]{1,0:T(4,128)S(1)}, f32[4,32,128]{2,1,0:T(8,128)S(1)}) custom-call(f32[4,32,128]{2,1,0:T(8,128)} %v_hbm.1, f32[4,32,128]{2,1,0:T(8,128)} %m_hbm.1, bf16[4,4,32,128]{3,2,1,0:T(8,128)(2,1)} %bg_hbm.1, s32[3,256]{1,0:T(4,128)} %rec_hbm.1, s32[16]{0:T(128)} %ck_hbm.1), custom_call_target="tpu_custom_call" | custom-call | tf_op jit(solution)/shard_map/pallas_call | solution.py:724
  56.3 0.7 %shard_map.85 = (f32[4,32,128]{2,1,0:T(8,128)}, f32[16,256]{1,0:T(8,128)}, f32[4,32]{1,0:T(4,128)}, f32[4,32,128]{2,1,0:T(8,128)}) custom-call(f32[4,32,128]{2,1,0:T(8,128)S(1)} %get-tuple-element.8.refs_0_, f32[16,256]{1,0:T(8,128)S(1)} %get-tuple-element.9.refs_1_, f32[4,32]{1,0:T(4,128)S(1)} %get-tuple-element.10.refs_2_, ...), custom_call_target="tpu_custom_call" | custom-call | tf_op jit(solution)/shard_map/pallas_call | solution.py:779

commit v4 on v3

--- a/solution.py
+++ b/solution.py
@@ -313,21 +313,22 @@
 
     lax.fori_loop(0, rows, wait_in, 0)
 
-    def gathered(f, z):
-        low = landed[pl.ds(f * nz + z, gxs, stride=gys * slab), :]
-        high = landed[pl.ds(slab + f * nz + z, gxs, stride=gys * slab), :]
+    def gathered(f):
+        low, high = (
+            jnp.stack([landed[pl.ds(g * slab + f * nz + z, gxs, stride=gys * slab), :] for z in range(nz)])
+            for g in range(gys)
+        )
         return plane.join(low, high)
 
-    for z in range(nz):
-        vs = gathered(0, z)
-        ms = gathered(1, z)
+    own = slice(nz, 2 * nz)
+    vs, ms = gathered(0), gathered(1)
+    for c in range(2):
+        vel[own, c] = far_coef * vs[c]
+    for k in range(nck):
+        accel = gathered(2 + k)
         for c in range(2):
-            vel[nz + z, c] = far_coef * vs[c]
-        for k in range(nck):
-            accel = gathered(2 + k, z)
-            for c in range(2):
-                own_bg[k, z, c] = accel[c]
-                src[k, nz + z, c] = ms[c] * accel[c]
+            own_bg[k, :, c] = accel[c]
+            src[k, own, c] = ms[c] * accel[c]
 
     halo = 2 * BLOCK
     soon, rest = halo // 4, halo // 2
@@ -595,10 +596,10 @@
             lines.append(jnp.sum(at_row * picked, axis=0, keepdims=True))
         return jnp.concatenate(lines, axis=0)
 
-    def give_back(read, dst):
-        for z in range(nz):
-            for g, value in enumerate(plane.split(*read(z))):
-                dst[pl.ds(g * nz + z, gxs, stride=gys * nz), :] = value
+    def give_back(field, dst):
+        for g, value in enumerate(plane.split(field[:, 0], field[:, 1])):
+            for z in range(nz):
+                dst[pl.ds(g * nz + z, gxs, stride=gys * nz), :] = value[z]
 
     last = steps - 1
     forward_step(last, halo - 2)
@@ -610,7 +611,7 @@
     adjoint_step(last - 3, 0)
     newer = newer_copies(blocks, adj.at[last - 3])
     launch(newer)
-    give_back(lambda z: (hist[last, nz + z, 0], hist[last, nz + z, 1]), back_w)
+    give_back(hist[last, own], back_w)
     send_back(back_w, in_w, s_w, r_w, lax.rem(pos, per), owner)
     part[0] = gather_traces()
     tr1[seat] = part[0]
@@ -647,7 +648,7 @@
     for b in range(1, blocks):
         adjoint_block(b)
 
-    give_back(lambda z: (img[z, 0], img[z, 1]), back_i)
+    give_back(img[...], back_i)
     send_back(back_i, in_i, s_i, r_i, lax.rem(pos, per), owner)
     trace_waits(part.at[1], tr2, 1)
     total = tr2[0]

time: 57.2 us -> 57.2 us (level)
  no operation moved by 1% of the time
where the time goes in v4:
time: 57.2 us; the launch traced here: 57.1 us
  Pallas kernels  56.4 us (99%)
  between operations  0.64 us (1%)
    pallas_call x1, Pallas kernels, chain_on_device(): pl.pallas_call(functools.partial(chain_kernel, dims), out_shape=shapes, i...  55.7 us

profile of v4, /device:TPU:0, one launch (start us, length us, event | category | flops | bytes accessed | tf_op | source)
XLA Modules:
  0.0 57.1 jit_solution(5185276947556411897)
XLA Ops:
  0.6 55.7 %shard_map.84 = (f32[4,32,128]{2,1,0:T(8,128)S(1)}, f32[16,256]{1,0:T(8,128)S(1)}, f32[4,32]{1,0:T(4,128)S(1)}, f32[4,32,128]{2,1,0:T(8,128)S(1)}) custom-call(f32[4,32,128]{2,1,0:T(8,128)} %v_hbm.1, f32[4,32,128]{2,1,0:T(8,128)} %m_hbm.1, bf16[4,4,32,128]{3,2,1,0:T(8,128)(2,1)} %bg_hbm.1, s32[3,256]{1,0:T(4,128)} %rec_hbm.1, s32[16]{0:T(128)} %ck_hbm.1), custom_call_target="tpu_custom_call" | custom-call | tf_op jit(solution)/shard_map/pallas_call | solution.py:725
  56.4 0.7 %shard_map.85 = (f32[4,32,128]{2,1,0:T(8,128)}, f32[16,256]{1,0:T(8,128)}, f32[4,32]{1,0:T(4,128)}, f32[4,32,128]{2,1,0:T(8,128)}) custom-call(f32[4,32,128]{2,1,0:T(8,128)S(1)} %get-tuple-element.8.refs_0_, f32[16,256]{1,0:T(8,128)S(1)} %get-tuple-element.9.refs_1_, f32[4,32]{1,0:T(4,128)S(1)} %get-tuple-element.10.refs_2_, ...), custom_call_target="tpu_custom_call" | custom-call | tf_op jit(solution)/shard_map/pallas_call | solution.py:780
